TPU v7x, 32 devices: a whole 2x2x4 slice. The times are simulated.
32 devices in a mesh: row: 4 (over y, x), col: 4 (over z), depth: 2 (over core).
Axes of the slice: x: 2, y: 2, z: 4, core: 2. Of those that a mesh axis runs over, the one named last changes fastest.
Arguments:
- layers: float32 [2, 4096, 4096], P('depth', 'row', 'col'), may hold values from -3 to 134.2, as said below
Outputs:
- factor: float32 [2, 4096, 512], P(None, 'row', 'depth')
- schur: float32 [4096, 4096], P(('row', 'depth'), 'col')
Inputs may be any that keep to these rules, and one draw needn't show every extreme that they name: Read in matrix order, each layer is symmetric, and the sum over layers is symmetric positive definite with a diagonal of order sqrt(4096).
All inputs are finite; a program needn't handle non-finite values.
Results may differ from a plain program's by a relative error of at most 0.0001.
Values sent between devices are 32-bit elements; how exact they have to be, the bound alone decides.
A program may use at most 192 MiB of HBM per device.

v0:
```python
import functools

import jax
import jax.numpy as jnp
from jax import lax
from jax.experimental import pallas as pl
from jax.experimental.pallas import tpu as pltpu
from jax.sharding import PartitionSpec as P

PANEL = 512
PANELS = 2
INNER = 128
STRIP = 8
HIGH = lax.Precision.HIGH
HIGHEST = lax.Precision.HIGHEST


def dot(a, b, ca, cb, precision):
    return lax.dot_general(
        a, b, (((ca,), (cb,)), ((), ())), precision=precision, preferred_element_type=jnp.float32
    )


def factor_strip(work, inv, strip):
    first = pl.multiple_of(strip * STRIP, STRIP)
    rows = work[pl.ds(first, STRIP), :]
    irows = inv[pl.ds(first, STRIP), :]
    rolled = pltpu.roll(rows, (INNER - first) % INNER, 1)
    sub = lax.broadcasted_iota(jnp.int32, (STRIP, INNER), 0)
    lane = lax.broadcasted_iota(jnp.int32, (STRIP, INNER), 1)
    cols = [jnp.broadcast_to(rolled[:, t : t + 1], (STRIP, INNER)) for t in range(STRIP)]
    pivots = jnp.zeros((STRIP, INNER), jnp.float32)
    for t in range(STRIP):
        pivot = jnp.broadcast_to(cols[t][t : t + 1, :], (STRIP, INNER))
        pivots = jnp.where(sub == t, pivot, pivots)
        if t + 1 < STRIP:
            mult = jnp.where(sub > t, cols[t] * (1.0 / pivot), 0.0)
            for s in range(t + 1, STRIP):
                cols[s] = cols[s] - mult * jnp.broadcast_to(cols[s][t : t + 1, :], (STRIP, INNER))
            rows = rows - mult * jnp.broadcast_to(rows[t : t + 1, :], (STRIP, INNER))
            irows = irows - mult * jnp.broadcast_to(irows[t : t + 1, :], (STRIP, INNER))
    scale = lax.rsqrt(pivots)
    rows = rows * scale
    irows = irows * scale
    inv[pl.ds(first, STRIP), :] = irows
    below = jnp.where(lane >= first + STRIP, rows, 0.0)
    update = dot(below, jnp.concatenate([rows, irows], axis=1), 0, 0, HIGHEST)
    work[...] -= update[:, :INNER]
    inv[...] -= update[:, INNER:]


def inverse_kernel(block_ref, out_ref, whole, work, inv):
    size = block_ref.shape[0]
    whole[...] = block_ref[...]
    eye = (
        lax.broadcasted_iota(jnp.int32, (INNER, INNER), 0)
        == lax.broadcasted_iota(jnp.int32, (INNER, INNER), 1)
    ).astype(jnp.float32)
    out_ref[...] = jnp.zeros_like(out_ref)
    for k in range(size // INNER):
        lo, hi = k * INNER, (k + 1) * INNER
        work[...] = whole[lo:hi, lo:hi]
        inv[...] = eye

        def step(strip, carry):
            factor_strip(work, inv, strip)
            return carry

        lax.fori_loop(0, INNER // STRIP, step, 0)
        corner = inv[...]
        if k:
            out_ref[lo:hi, :lo] = dot(corner, out_ref[lo:hi, :lo], 1, 0, HIGHEST)
        out_ref[lo:hi, lo:hi] = corner
        if hi < size:
            below = dot(whole[hi:, lo:hi], corner, 1, 1, HIGHEST)
            whole[hi:, hi:] -= dot(below, below, 1, 1, HIGHEST)
            out_ref[hi:, :hi] -= dot(below, out_ref[lo:hi, :hi], 1, 0, HIGHEST)


def block_inverse(block):
    size = block.shape[0]
    return pl.pallas_call(
        inverse_kernel,
        out_shape=jax.ShapeDtypeStruct((size, size), jnp.float32),
        in_specs=[pl.BlockSpec(memory_space=pltpu.VMEM)],
        out_specs=pl.BlockSpec(memory_space=pltpu.VMEM),
        scratch_shapes=[
            pltpu.VMEM((size, size), jnp.float32),
            pltpu.VMEM((INNER, INNER), jnp.float32),
            pltpu.VMEM((INNER, INNER), jnp.float32),
        ],
        cost_estimate=pl.CostEstimate(flops=2 * size**3, bytes_accessed=8 * size**2, transcendentals=size),
        name="block_inverse",
    )(block)


def pick(index, table):
    value = 0
    for i, entry in enumerate(table):
        value = value + jnp.where(index == i, entry, 0)
    return value


def spread_kernel(groups, s_ref, rowp, colp, diag, zrecv, zsend, rrecv, rsend, srecv, ssend, lsem):
    row_groups, col_groups = groups
    r, c, d = lax.axis_index("row"), lax.axis_index("col"), lax.axis_index("depth")
    z_chunks, chunks = zrecv.shape[1], rrecv.shape[1]
    ring = list(range(row_groups))
    if row_groups & (row_groups - 1) == 0:
        ring = [i ^ (i >> 1) for i in ring]
    place = [ring.index(i) for i in range(row_groups)]
    pos = pick(r, place)
    after = pick(r, [ring[(place[i] + 1) % row_groups] for i in range(row_groups)])
    before = pick(r, [ring[(place[i] - 1) % row_groups] for i in range(row_groups)])
    target = jnp.where(d == 0, after, before)
    half = PANEL // 2
    last = []

    def local(src, dst):
        copy = pltpu.make_async_copy(src, dst, lsem)
        copy.start()
        copy.wait()

    def line(p, k):
        root, lane = p % col_groups, (p // col_groups) * PANEL
        size = PANEL // z_chunks
        rows = pl.ds(k * size, size)
        block = rowp.at[p, rows]

        def copy(way):
            return pltpu.make_async_remote_copy(
                src_ref=block,
                dst_ref=block,
                send_sem=zsend.at[p, k, max(way, 0)],
                recv_sem=zrecv.at[p, k],
                device_id={"col": c + way},
                device_id_type=pl.DeviceIdType.MESH,
            )

        @pl.when(c == root)
        def _():
            local(s_ref.at[rows, pl.ds(lane, PANEL)], block)

        @pl.when(c != root)
        def _():
            copy(1).wait_recv()

        up, down = (c >= root) & (c < col_groups - 1), (c <= root) & (c > 0)

        @pl.when(up)
        def _():
            copy(1).start()

        @pl.when(down)
        def _():
            copy(-1).start()

        def finish():
            @pl.when(up)
            def _():
                copy(1).wait_send()

            @pl.when(down)
            def _():
                copy(-1).wait_send()

        last.append(finish)

    def around(item, root, owner, src, dst, k):
        start = place[root]
        rel = jnp.where(d == 0, (pos - start + row_groups) % row_groups, (start - pos + row_groups) % row_groups)
        size = half // chunks
        own = pl.ds(pl.multiple_of(d * half + k * size, size), size)
        other = pl.ds(pl.multiple_of((1 - d) * half + k * size, size), size)
        is_root = rel == 0
        sends = rel < row_groups - 1
        origin = is_root & (d == owner)

        def hop():
            return pltpu.make_async_remote_copy(
                src_ref=dst.at[own],
                dst_ref=dst.at[own],
                send_sem=rsend.at[item, k],
                recv_sem=rrecv.at[item, k],
                device_id={"row": target},
                device_id_type=pl.DeviceIdType.MESH,
            )

        def across(kind):
            block = dst.at[(own, other)[kind]]
            return pltpu.make_async_remote_copy(
                src_ref=block,
                dst_ref=block,
                send_sem=ssend.at[item, kind, k],
                recv_sem=srecv.at[item, kind, k],
                device_id={"depth": 1 - d},
                device_id_type=pl.DeviceIdType.MESH,
            )

        @pl.when(origin)
        def _():
            local(src.at[other], dst.at[other])
            across(1).start()
            local(src.at[own], dst.at[own])
            across(0).start()

        @pl.when(is_root & (d != owner))
        def _():
            across(1).wait_recv()

        @pl.when(rel > 0)
        def _():
            hop().wait_recv()

        @pl.when(sends)
        def _():
            hop().start()

        @pl.when(rel > 0)
        def _():
            across(0).start()

        def finish():
            @pl.when(origin)
            def _():
                across(1).wait_send()
                across(0).wait_send()

            @pl.when(jnp.logical_not(origin))
            def _():
                across(0).wait_recv()

            @pl.when(rel > 0)
            def _():
                across(0).wait_send()

            @pl.when(sends)
            def _():
                hop().wait_send()

        last.append(finish)

    def owner_of(p):
        return p % row_groups, p // row_groups

    pairs = [(p, q) for p in range(PANELS) for q in range(p + 1)]
    order = [k for j in range(z_chunks // 2) for k in (j, j + z_chunks // 2)]
    for p in range(PANELS):
        for j in range(max(z_chunks, chunks)):
            if j < z_chunks:
                line(p, order[j])
            if j < chunks:
                around(len(pairs) + p, *owner_of(p), s_ref, colp.at[p], j)
        for item, (a, b) in enumerate(pairs):
            if b == p:
                for k in range(chunks):
                    around(item, *owner_of(a), rowp.at[b], diag.at[item], k)
    for finish in last:
        finish()


def spread(summed, row_groups, col_groups):
    cols = summed.shape[1]
    z_chunks, chunks = 8, 8
    blocks = PANELS * (PANELS + 1) // 2
    items = blocks + PANELS
    dma = pltpu.SemaphoreType.DMA
    vmem = pl.BlockSpec(memory_space=pltpu.VMEM)
    return pl.pallas_call(
        functools.partial(spread_kernel, (row_groups, col_groups)),
        out_shape=(
            jax.ShapeDtypeStruct((PANELS, PANEL, PANEL), jnp.float32),
            jax.ShapeDtypeStruct((PANELS, PANEL, cols), jnp.float32),
            jax.ShapeDtypeStruct((blocks, PANEL, PANEL), jnp.float32),
        ),
        in_specs=[vmem],
        out_specs=(vmem, vmem, vmem),
        scratch_shapes=[
            dma((PANELS, z_chunks)),
            dma((PANELS, z_chunks, 2)),
            dma((items, chunks)),
            dma((items, chunks)),
            dma((items, 2, chunks)),
            dma((items, 2, chunks)),
            dma,
        ],
        compiler_params=pltpu.CompilerParams(has_side_effects=True, vmem_limit_bytes=60 * 1024 * 1024),
        name="spread",
    )(summed)


def per_device(layers):
    row_groups = lax.axis_size("row")
    col_groups = lax.axis_size("col")
    depth_groups = lax.axis_size("depth")
    row = lax.axis_index("row")
    col = lax.axis_index("col")
    depth = lax.axis_index("depth")
    layer = layers[0]
    cols_local = layer.shape[1]
    assert layer.shape[0] == PANEL * depth_groups and depth_groups == 2

    swap = [(0, 1), (1, 0)]
    mine = lax.dynamic_slice_in_dim(layer, depth * PANEL, PANEL, 0)
    theirs = lax.dynamic_slice_in_dim(layer, (1 - depth) * PANEL, PANEL, 0)
    summed = mine + lax.ppermute(theirs, "depth", swap)
    own_block = row + row_groups * depth
    col_block = jnp.arange(cols_local, dtype=jnp.int32) // PANEL * col_groups + col

    rowp, colp, diag = spread(summed, row_groups, col_groups)
    rows = [rowp[p] for p in range(PANELS)]
    cols = [colp[p] for p in range(PANELS)]
    pairs = [(p, q) for p in range(PANELS) for q in range(p + 1)]
    lead = {pair: diag[i] for i, pair in enumerate(pairs)}
    factors, left, right = [], [], []
    for p in range(PANELS):
        inverse = block_inverse(lead[p, p])
        solved = {a: dot(lead[a, p], inverse, 1, 1, HIGHEST) for a in range(p + 1, PANELS)}
        for a in range(p + 1, PANELS):
            for b in range(p + 1, a + 1):
                lead[a, b] = lead[a, b] - dot(solved[a], solved[b], 1, 1, HIGHEST)
        c_rows = jnp.where(own_block >= p, dot(rows[p], inverse, 1, 1, HIGH), 0.0)
        below = jnp.where(own_block > p, c_rows, 0.0)
        c_cols = dot(inverse, cols[p], 1, 0, HIGH)
        c_cols = jnp.where((col_block > p)[None, :], c_cols, 0.0)
        factors.append(c_rows)
        left.append(below)
        right.append(c_cols)
        for q in range(p + 1, PANELS):
            rows[q] = rows[q] - dot(below, solved[q], 1, 1, HIGH)
            cols[q] = cols[q] - dot(solved[q], c_cols, 1, 0, HIGH)
    update = dot(jnp.concatenate(left, 1), jnp.concatenate(right, 0), 1, 0, HIGH)
    schur = summed - update
    factor = jnp.stack(factors)
    width = PANEL // depth_groups
    kept = lax.dynamic_slice_in_dim(factor, depth * width, width, 2)
    sent = lax.dynamic_slice_in_dim(factor, (1 - depth) * width, width, 2)
    got = lax.ppermute(sent, "depth", swap)
    first = jnp.where(depth == 0, kept, got)
    second = jnp.where(depth == 0, got, kept)
    return jnp.concatenate([first, second], axis=1), schur


def solution(mesh):
    return jax.shard_map(
        per_device,
        mesh=mesh,
        in_specs=(P("depth", "row", "col"),),
        out_specs=(P(None, "row", "depth"), P(("row", "depth"), "col")),
        check_vma=False,
    )
```

profile of v0, /device:TPU:28, one launch (start us, length us, event | category | flops | bytes accessed | tf_op | source)
XLA Modules:
  0.0 218.8 jit_solution(2592359504931075520)
XLA Ops:
  0.6 3.2 %dynamic-slice_bitcast_fusion = f32[512,1024]{1,0:T(8,128)} fusion(f32[1,1024,1024]{2,1,0:T(8,128)} %param.1, s32[]{:T(128)S(6)} %select_n.72), kind=kLoop, calls=%fused_computation.19 | loop fusion | bytes 4194308 | tf_op jit(solution)/shard_map/dynamic_slice | solution.py:305
  3.8 0.0 collective-permute-start
  3.8 4.3 %collective-permute-done = f32[512,1024]{1,0:T(8,128)S(1)} collective-permute-done((f32[512,1024]{1,0:T(8,128)}, f32[512,1024]{1,0:T(8,128)S(1)}, u32[]{:S(2)}, u32[]{:S(2)}) %collective-permute-start) | collective-permute-done | bytes 2097184 | tf_op jit(solution)/shard_map/ppermute | solution.py:306
  8.2 3.3 %bitcast_add_fusion.s_ref = f32[512,1024]{1,0:T(8,128)} fusion(f32[512,1024]{1,0:T(8,128)S(1)} %collective-permute-done, f32[1,1024,1024]{2,1,0:T(8,128)} %param.1, s32[]{:T(128)S(6)} %select_n.71), kind=kLoop, calls=%fused_computation.16 | loop fusion | flops 524288 | bytes 6291460 | tf_op jit(solution)/shard_map/add | solution.py:306
  11.5 95.5 %spread.1 = (f32[2,512,512]{2,1,0:T(8,128)}, f32[2,512,1024]{2,1,0:T(8,128)}, f32[3,512,512]{2,1,0:T(8,128)}) custom-call(f32[512,1024]{1,0:T(8,128)} %bitcast_add_fusion.s_ref), custom_call_target="tpu_custom_call" | custom-call | tf_op jit(solution)/shard_map/spread/pallas_call | solution.py:269
  106.9 2.3 %slice_bitcast_fusion.block_ref = f32[512,512]{1,0:T(8,128)} fusion(f32[3,512,512]{2,1,0:T(8,128)} %get-tuple-element.6), kind=kLoop, calls=%fused_computation.33 | loop fusion | bytes 2097152 | tf_op jit(solution)/shard_map/squeeze | solution.py:314
  109.2 41.2 %block_inverse.2 = f32[512,512]{1,0:T(8,128)} custom-call(f32[512,512]{1,0:T(8,128)} %slice_bitcast_fusion.block_ref), custom_call_target="tpu_custom_call" | custom-call | flops 268435456 | bytes 2097152 | tf_op jit(solution)/shard_map/block_inverse/pallas_call | solution.py:82
  150.5 3.4 %fusion.18 = f32[512,512]{1,0:T(8,128)S(1)} fusion(f32[512,512]{1,0:T(8,128)} %block_inverse.2, f32[3,512,512]{2,1,0:T(8,128)} %get-tuple-element.6), kind=kOutput, calls=%fused_computation.27 | convolution fusion | flops 1610612736 | bytes 3145728 | tf_op jit(solution)/shard_map/dot_general | solution.py:19
  153.9 4.1 %bitcast_subtract_fusion.4.block_ref = f32[512,512]{1,0:T(8,128)} fusion(f32[3,512,512]{2,1,0:T(8,128)} %get-tuple-element.6, f32[512,512]{1,0:T(8,128)S(1)} %fusion.18), kind=kOutput, calls=%fused_computation.26 | convolution fusion | flops 1610874880 | bytes 4194304 | tf_op jit(solution)/shard_map/dot_general | solution.py:19
  157.9 0.0 copy-start.1
  157.9 41.6 %block_inverse.3 = f32[512,512]{1,0:T(8,128)} custom-call(f32[512,512]{1,0:T(8,128)} %bitcast_subtract_fusion.4.block_ref), custom_call_target="tpu_custom_call" | custom-call | flops 268435456 | bytes 2097152 | tf_op jit(solution)/shard_map/block_inverse/pallas_call | solution.py:82
  199.5 0.0 copy-done.1
  199.5 2.3 %broadcast_select_fusion.1 = (f32[512,512]{1,0:T(8,128)S(1)}, f32[512,512]{1,0:T(8,128)S(1)}) fusion(pred[]{:T(512)S(6)} %gt.22, f32[512,512]{1,0:T(8,128)S(1)} %copy-done.1, f32[2,512,512]{2,1,0:T(8,128)} %get-tuple-element.5, pred[]{:T(512)S(6)} %ge.6), kind=kOutput, calls=%fused_computation.37 | convolution fusion | flops 805830656 | bytes 4194306 | tf_op jit(solution)/shard_map/dot_general | solution.py:19
  201.8 0.0 copy-start.2
  201.8 0.0 copy-start.4
  201.8 1.0 fusion.37
  202.8 0.2 copy-done.2
  203.0 0.7 copy-done.4
  203.7 0.0 copy-start.3
  203.7 1.1 broadcast_select_fusion
  204.8 0.1 fusion.16
  204.9 1.2 collective-permute-start.1
  206.1 0.0 copy-done.3
  206.1 1.9 fusion.12
  208.1 1.9 fusion.38
  210.0 0.0 copy-start
  210.0 1.9 fusion.15
  211.9 0.0 copy-done
  211.9 5.2 %fusion.24 = f32[512,1024]{1,0:T(8,128)} fusion(f32[512,1024]{1,0:T(8,128)S(1)} %copy-done, f32[512,1024]{1,0:T(8,128)S(1)} %fusion.15, f32[512,1024]{1,0:T(8,128)S(1)} %fusion.12, f32[512,512]{1,0:T(8,128)S(1)} %get-tuple-element.12, f32[512,512]{1,0:T(8,128)S(1)} %get-tuple-element.10), kind=kOutput, calls=%fused_computation.35 | convolution fusion | flops 3223322624 | bytes 10485760 | tf_op jit(solution)/shard_map/dot_general | solution.py:19
  217.1 0.0 collective-permute-done.1
  217.1 0.2 broadcast_select_fusion.3
  217.3 1.5 pad_maximum_fusion
  (2 shorter events, 0.0 us)
Async XLA Ops:
  3.8 4.4 %collective-permute-start = (f32[512,1024]{1,0:T(8,128)}, f32[512,1024]{1,0:T(8,128)S(1)}, u32[]{:S(2)}, u32[]{:S(2)}) collective-permute-start(f32[512,1024]{1,0:T(8,128)} %dynamic-slice_bitcast_fusion), channel_id=1, source_target_pairs={{0,1},{1,0},{2,3},{3,2},{4,5},{5,4},{6,7},{7,6},{8,9},{9,8},{10,11... | collective-permute-start | bytes 6291464 | tf_op jit(solution)/shard_map/ppermute | solution.py:306
  157.9 41.6 %copy-start.1 = (f32[512,512]{1,0:T(8,128)S(1)}, f32[512,512]{1,0:T(8,128)}, u32[]{:S(2)}) copy-start(f32[512,512]{1,0:T(8,128)} %block_inverse.2) | copy-start | bytes 3145732
  201.8 1.2 copy-start.2
  201.8 1.9 copy-start.4
  203.7 2.4 %copy-start.3 = (f32[2,512,1024]{2,1,0:T(8,128)S(1)}, f32[2,512,1024]{2,1,0:T(8,128)}, u32[]{:S(2)}) copy-start(f32[2,512,1024]{2,1,0:T(8,128)} %get-tuple-element.7) | copy-start | bytes 12582916
  204.9 12.2 %collective-permute-start.1 = (f32[2,512,256]{2,1,0:T(8,128)S(1)}, f32[2,512,256]{2,1,0:T(8,128)S(1)}, u32[]{:S(2)}, u32[]{:S(2)}) collective-permute-start(f32[2,512,256]{2,1,0:T(8,128)S(1)} %fusion.16), channel_id=1, source_target_pairs={{0,1},{1,0},{2,3},{3,2},{4,5},{5,4},{6,7},{7,6},{8,9},{9,8},{10,11... | collective-permute-start | bytes 3145736 | tf_op jit(solution)/shard_map/ppermute | solution.py:338
  210.0 1.9 copy-start
where the time goes:
time: 222 us; the launch traced here: 219 us
  Pallas kernels  178 us (80%)
  matrix products  22.8 us (10%)
  local copies, waits for them, and re-layouts  6.3 us (3%)
  other arithmetic  5.08 us (2%)
  waiting for transfers between devices  4.35 us (2%)
    pallas_call x1, Pallas kernels, spread(): pl.pallas_call(functools.partial(spread_kernel, (row_groups, col_groups))...  95.5 us
    pallas_call x2, Pallas kernels, block_inverse(): pl.pallas_call(inverse_kernel, out_shape=jax.ShapeDtypeStruct((size, size...  82.8 us
    dot_general x9, matrix products, dot(): lax.dot_general(a, b, (((ca,), (cb,)), ((), ())), precision=precision, pr...  22.8 us
  transfers between devices with their start and end apart: 2, of which 1 were waited for; matrix products, arithmetic and copies ran while one was open for 5% of the time, Pallas kernels for 0%

commit v1 on v0

--- a/solution.py
+++ b/solution.py
@@ -21,52 +21,54 @@
     )
 
 
-def factor_strip(work, inv, strip):
-    first = pl.multiple_of(strip * STRIP, STRIP)
-    rows = work[pl.ds(first, STRIP), :]
-    irows = inv[pl.ds(first, STRIP), :]
-    rolled = pltpu.roll(rows, (INNER - first) % INNER, 1)
-    sub = lax.broadcasted_iota(jnp.int32, (STRIP, INNER), 0)
-    lane = lax.broadcasted_iota(jnp.int32, (STRIP, INNER), 1)
-    cols = [jnp.broadcast_to(rolled[:, t : t + 1], (STRIP, INNER)) for t in range(STRIP)]
-    pivots = jnp.zeros((STRIP, INNER), jnp.float32)
-    for t in range(STRIP):
-        pivot = jnp.broadcast_to(cols[t][t : t + 1, :], (STRIP, INNER))
-        pivots = jnp.where(sub == t, pivot, pivots)
-        if t + 1 < STRIP:
-            mult = jnp.where(sub > t, cols[t] * (1.0 / pivot), 0.0)
+def tree(terms):
+    while len(terms) > 1:
+        terms = [terms[i] + terms[i + 1] if i + 1 < len(terms) else terms[i] for i in range(0, len(terms), 2)]
+    return terms[0]
+
+def factor_corner(work, inv):
+    shape = (STRIP, INNER)
+    sub = lax.broadcasted_iota(jnp.int32, shape, 0)
+    lane = lax.broadcasted_iota(jnp.int32, shape, 1)
+    def splat(x, t):
+        return jnp.broadcast_to(x[t:t+1, :], shape)
+    def column(x, j):
+        return jnp.broadcast_to(x[:, j:j+1], shape)
+    n = INNER // STRIP
+    m = [work[a*STRIP:(a+1)*STRIP, :] for a in range(n)]
+    for q in range(n):
+        lo = q * STRIP
+        panel = (lane >= lo) & (lane < lo + STRIP)
+        rows = m[q]
+        cols = [column(rows, lo + t) for t in range(STRIP)]
+        full = jnp.where(panel, jnp.where(lane == lo + sub, 1.0, 0.0), rows)
+        lower = full
+        pivots = None
+        for t in range(STRIP):
+            pivot = splat(cols[t], t)
+            pivots = pivot if pivots is None else jnp.where(sub >= t, pivot, pivots)
+            scaled = cols[t] * (1.0 / pivot)
+            both = jnp.where(sub == t, 0.0, scaled)
             for s in range(t + 1, STRIP):
-                cols[s] = cols[s] - mult * jnp.broadcast_to(cols[s][t : t + 1, :], (STRIP, INNER))
-            rows = rows - mult * jnp.broadcast_to(rows[t : t + 1, :], (STRIP, INNER))
-            irows = irows - mult * jnp.broadcast_to(irows[t : t + 1, :], (STRIP, INNER))
-    scale = lax.rsqrt(pivots)
-    rows = rows * scale
-    irows = irows * scale
-    inv[pl.ds(first, STRIP), :] = irows
-    below = jnp.where(lane >= first + STRIP, rows, 0.0)
-    update = dot(below, jnp.concatenate([rows, irows], axis=1), 0, 0, HIGHEST)
-    work[...] -= update[:, :INNER]
-    inv[...] -= update[:, INNER:]
-
+                cols[s] = cols[s] - both * splat(cols[s], t)
+            head = splat(full, t)
+            full = full - both * head
+            if t + 1 < STRIP:
+                lower = lower - jnp.where(sub > t, scaled, 0.0) * head
+        inv[lo:lo+STRIP, :] = jnp.where(lane < lo + STRIP, lower * lax.rsqrt(pivots), 0.0)
+        if q + 1 < n:
+            full = full * (1.0 / pivots)
+            heads = [splat(full, t) for t in range(STRIP)]
+            for a in range(q + 1, n):
+                parts = tree([column(m[a], lo + t) * heads[t] for t in range(STRIP)])
+                m[a] = jnp.where(panel, 0.0, m[a]) - parts
 
 def inverse_kernel(block_ref, out_ref, whole, work, inv):
     size = block_ref.shape[0]
     whole[...] = block_ref[...]
-    eye = (
-        lax.broadcasted_iota(jnp.int32, (INNER, INNER), 0)
-        == lax.broadcasted_iota(jnp.int32, (INNER, INNER), 1)
-    ).astype(jnp.float32)
     out_ref[...] = jnp.zeros_like(out_ref)
-    for k in range(size // INNER):
+    def update(k):
         lo, hi = k * INNER, (k + 1) * INNER
-        work[...] = whole[lo:hi, lo:hi]
-        inv[...] = eye
-
-        def step(strip, carry):
-            factor_strip(work, inv, strip)
-            return carry
-
-        lax.fori_loop(0, INNER // STRIP, step, 0)
         corner = inv[...]
         if k:
             out_ref[lo:hi, :lo] = dot(corner, out_ref[lo:hi, :lo], 1, 0, HIGHEST)
@@ -75,6 +77,16 @@
             below = dot(whole[hi:, lo:hi], corner, 1, 1, HIGHEST)
             whole[hi:, hi:] -= dot(below, below, 1, 1, HIGHEST)
             out_ref[hi:, :hi] -= dot(below, out_ref[lo:hi, :hi], 1, 0, HIGHEST)
+
+    def step(k, carry):
+        first = pl.ds(pl.multiple_of(k * INNER, INNER), INNER)
+        work[...] = whole[first, first]
+        factor_corner(work, inv)
+        for static in range(size // INNER):
+            pl.when(k == static)(functools.partial(update, static))
+        return carry
+
+    lax.fori_loop(0, size // INNER, step, 0)
 
 
 def block_inverse(block):

time: 222 us -> 186 us (0.84)
  Pallas kernels: 178 us -> 143 us
    pallas_call x2, Pallas kernels: 82.8 us -> 47.2 us  [block_inverse(): pl.pallas_call(inverse_kernel, out_shape=jax.ShapeDtypeStruct((size, size...]
  transfers between devices with their start and end apart: 2 -> 2, of which waited for: 1 -> 1; matrix products, arithmetic and copies ran while one was open for 5% -> 6% of each run, Pallas kernels for 0% -> 0%
where the time goes in v1:
time: 186 us; the launch traced here: 183 us
  Pallas kernels  143 us (77%)
  matrix products  22.8 us (12%)
  local copies, waits for them, and re-layouts  6.3 us (3%)
  other arithmetic  5.08 us (3%)
  waiting for transfers between devices  4.35 us (2%)
    pallas_call x1, Pallas kernels, spread(): pl.pallas_call(functools.partial(spread_kernel, (row_groups, col_groups))...  95.5 us
    pallas_call x2, Pallas kernels, block_inverse(): pl.pallas_call(inverse_kernel, out_shape=jax.ShapeDtypeStruct((size, size...  47.2 us
    dot_general x9, matrix products, dot(): lax.dot_general(a, b, (((ca,), (cb,)), ((), ())), precision=precision, pr...  22.8 us
    ppermute x1, waiting for transfers between devices, per_device(): summed = mine + lax.ppermute(theirs, 'depth', swap)  4.34 us
  transfers between devices with their start and end apart: 2, of which 1 were waited for; matrix products, arithmetic and copies ran while one was open for 6% of the time, Pallas kernels for 0%

profile of v1, /device:TPU:28, one launch (start us, length us, event | category | flops | bytes accessed | tf_op | source)
XLA Modules:
  0.0 183.2 jit_solution(15422285780678753582)
XLA Ops:
  0.6 3.2 %dynamic-slice_bitcast_fusion = f32[512,1024]{1,0:T(8,128)} fusion(f32[1,1024,1024]{2,1,0:T(8,128)} %param.1, s32[]{:T(128)S(6)} %select_n.72), kind=kLoop, calls=%fused_computation.19 | loop fusion | bytes 4194308 | tf_op jit(solution)/shard_map/dynamic_slice | solution.py:317
  3.8 0.0 collective-permute-start
  3.8 4.3 %collective-permute-done = f32[512,1024]{1,0:T(8,128)S(1)} collective-permute-done((f32[512,1024]{1,0:T(8,128)}, f32[512,1024]{1,0:T(8,128)S(1)}, u32[]{:S(2)}, u32[]{:S(2)}) %collective-permute-start) | collective-permute-done | bytes 2097184 | tf_op jit(solution)/shard_map/ppermute | solution.py:318
  8.2 3.3 %bitcast_add_fusion.s_ref = f32[512,1024]{1,0:T(8,128)} fusion(f32[512,1024]{1,0:T(8,128)S(1)} %collective-permute-done, f32[1,1024,1024]{2,1,0:T(8,128)} %param.1, s32[]{:T(128)S(6)} %select_n.71), kind=kLoop, calls=%fused_computation.16 | loop fusion | flops 524288 | bytes 6291460 | tf_op jit(solution)/shard_map/add | solution.py:318
  11.5 95.5 %spread.1 = (f32[2,512,512]{2,1,0:T(8,128)}, f32[2,512,1024]{2,1,0:T(8,128)}, f32[3,512,512]{2,1,0:T(8,128)}) custom-call(f32[512,1024]{1,0:T(8,128)} %bitcast_add_fusion.s_ref), custom_call_target="tpu_custom_call" | custom-call | tf_op jit(solution)/shard_map/spread/pallas_call | solution.py:281
  106.9 2.3 %slice_bitcast_fusion.block_ref = f32[512,512]{1,0:T(8,128)} fusion(f32[3,512,512]{2,1,0:T(8,128)} %get-tuple-element.6), kind=kLoop, calls=%fused_computation.33 | loop fusion | bytes 2097152 | tf_op jit(solution)/shard_map/squeeze | solution.py:326
  109.2 23.5 %block_inverse.2 = f32[512,512]{1,0:T(8,128)} custom-call(f32[512,512]{1,0:T(8,128)} %slice_bitcast_fusion.block_ref), custom_call_target="tpu_custom_call" | custom-call | flops 268435456 | bytes 2097152 | tf_op jit(solution)/shard_map/block_inverse/pallas_call | solution.py:94
  132.7 3.4 %fusion.18 = f32[512,512]{1,0:T(8,128)S(1)} fusion(f32[512,512]{1,0:T(8,128)} %block_inverse.2, f32[3,512,512]{2,1,0:T(8,128)} %get-tuple-element.6), kind=kOutput, calls=%fused_computation.27 | convolution fusion | flops 1610612736 | bytes 3145728 | tf_op jit(solution)/shard_map/dot_general | solution.py:19
  136.1 4.1 %bitcast_subtract_fusion.4.block_ref = f32[512,512]{1,0:T(8,128)} fusion(f32[3,512,512]{2,1,0:T(8,128)} %get-tuple-element.6, f32[512,512]{1,0:T(8,128)S(1)} %fusion.18), kind=kOutput, calls=%fused_computation.26 | convolution fusion | flops 1610874880 | bytes 4194304 | tf_op jit(solution)/shard_map/dot_general | solution.py:19
  140.1 0.0 copy-start.1
  140.1 23.8 %block_inverse.3 = f32[512,512]{1,0:T(8,128)} custom-call(f32[512,512]{1,0:T(8,128)} %bitcast_subtract_fusion.4.block_ref), custom_call_target="tpu_custom_call" | custom-call | flops 268435456 | bytes 2097152 | tf_op jit(solution)/shard_map/block_inverse/pallas_call | solution.py:94
  163.9 0.0 copy-done.1
  163.9 2.3 %broadcast_select_fusion.1 = (f32[512,512]{1,0:T(8,128)S(1)}, f32[512,512]{1,0:T(8,128)S(1)}) fusion(pred[]{:T(512)S(6)} %gt.22, f32[512,512]{1,0:T(8,128)S(1)} %copy-done.1, f32[2,512,512]{2,1,0:T(8,128)} %get-tuple-element.5, pred[]{:T(512)S(6)} %ge.6), kind=kOutput, calls=%fused_computation.37 | convolution fusion | flops 805830656 | bytes 4194306 | tf_op jit(solution)/shard_map/dot_general | solution.py:19
  166.2 0.0 copy-start.2
  166.2 0.0 copy-start.4
  166.2 1.0 fusion.37
  167.2 0.2 copy-done.2
  167.4 0.7 copy-done.4
  168.1 0.0 copy-start.3
  168.1 1.1 broadcast_select_fusion
  169.2 0.1 fusion.16
  169.3 1.2 collective-permute-start.1
  170.5 0.0 copy-done.3
  170.5 1.9 %fusion.12 = f32[512,1024]{1,0:T(8,128)S(1)} fusion(f32[512,512]{1,0:T(8,128)S(1)} %copy-done.1, f32[2,512,1024]{2,1,0:T(8,128)S(1)} %copy-done.3, pred[1024]{0:T(1024)(128)(4,1)S(1)} %fusion.34), kind=kOutput, calls=%fused_computation.20 | convolution fusion | flops 1611137024 | bytes 5243904 | tf_op jit(solution)/shard_map/dot_general | solution.py:19
  172.5 1.9 %fusion.38 = f32[512,1024]{1,0:T(8,128)S(1)} fusion(f32[512,512]{1,0:T(8,128)S(1)} %fusion.18, f32[512,1024]{1,0:T(8,128)S(1)} %fusion.12), kind=kOutput, calls=%fused_computation.53 | convolution fusion | flops 1610612736 | bytes 5242880 | tf_op jit(solution)/shard_map/dot_general | solution.py:19
  174.4 0.0 copy-start
  174.4 1.9 %fusion.15 = f32[512,1024]{1,0:T(8,128)S(1)} fusion(f32[512,512]{1,0:T(8,128)S(1)} %copy-done.2, f32[512,1024]{1,0:T(8,128)S(1)} %fusion.38, f32[2,512,1024]{2,1,0:T(8,128)S(1)} %copy-done.3, pred[1024]{0:T(1024)(128)(4,1)S(1)} %fusion.33), kind=kOutput, calls=%fused_computation.21 | convolution fusion | flops 1611661312 | bytes 7341056 | tf_op jit(solution)/shard_map/dot_general | solution.py:19
  176.3 0.0 copy-done
  176.3 5.2 %fusion.24 = f32[512,1024]{1,0:T(8,128)} fusion(f32[512,1024]{1,0:T(8,128)S(1)} %copy-done, f32[512,1024]{1,0:T(8,128)S(1)} %fusion.15, f32[512,1024]{1,0:T(8,128)S(1)} %fusion.12, f32[512,512]{1,0:T(8,128)S(1)} %get-tuple-element.12, f32[512,512]{1,0:T(8,128)S(1)} %get-tuple-element.10), kind=kOutput, calls=%fused_computation.35 | convolution fusion | flops 3223322624 | bytes 10485760 | tf_op jit(solution)/shard_map/dot_general | solution.py:19
  181.5 0.0 collective-permute-done.1
  181.5 0.2 broadcast_select_fusion.3
  181.7 1.5 pad_maximum_fusion
  (2 shorter events, 0.0 us)
Async XLA Ops:
  3.8 4.4 %collective-permute-start = (f32[512,1024]{1,0:T(8,128)}, f32[512,1024]{1,0:T(8,128)S(1)}, u32[]{:S(2)}, u32[]{:S(2)}) collective-permute-start(f32[512,1024]{1,0:T(8,128)} %dynamic-slice_bitcast_fusion), channel_id=1, source_target_pairs={{0,1},{1,0},{2,3},{3,2},{4,5},{5,4},{6,7},{7,6},{8,9},{9,8},{10,11... | collective-permute-start | bytes 6291464 | tf_op jit(solution)/shard_map/ppermute | solution.py:318
  140.1 23.8 %copy-start.1 = (f32[512,512]{1,0:T(8,128)S(1)}, f32[512,512]{1,0:T(8,128)}, u32[]{:S(2)}) copy-start(f32[512,512]{1,0:T(8,128)} %block_inverse.2) | copy-start | bytes 3145732
  166.2 1.2 copy-start.2
  166.2 1.9 %copy-start.4 = (f32[2,512,512]{2,1,0:T(8,128)S(1)}, f32[2,512,512]{2,1,0:T(8,128)}, u32[]{:S(2)}) copy-start(f32[2,512,512]{2,1,0:T(8,128)} %get-tuple-element.5) | copy-start | bytes 6291460
  168.1 2.4 %copy-start.3 = (f32[2,512,1024]{2,1,0:T(8,128)S(1)}, f32[2,512,1024]{2,1,0:T(8,128)}, u32[]{:S(2)}) copy-start(f32[2,512,1024]{2,1,0:T(8,128)} %get-tuple-element.7) | copy-start | bytes 12582916
  169.3 12.2 %collective-permute-start.1 = (f32[2,512,256]{2,1,0:T(8,128)S(1)}, f32[2,512,256]{2,1,0:T(8,128)S(1)}, u32[]{:S(2)}, u32[]{:S(2)}) collective-permute-start(f32[2,512,256]{2,1,0:T(8,128)S(1)} %fusion.16), channel_id=1, source_target_pairs={{0,1},{1,0},{2,3},{3,2},{4,5},{5,4},{6,7},{7,6},{8,9},{9,8},{10,11... | collective-permute-start | bytes 3145736 | tf_op jit(solution)/shard_map/ppermute | solution.py:350
  174.4 1.9 %copy-start = (f32[512,1024]{1,0:T(8,128)S(1)}, f32[512,1024]{1,0:T(8,128)}, u32[]{:S(2)}) copy-start(f32[512,1024]{1,0:T(8,128)} %bitcast_add_fusion.s_ref) | copy-start | bytes 6291460

commit v2 on v1

v2 whole, which is shorter than its diff:
```python
import functools

import jax
import jax.numpy as jnp
from jax import lax
from jax.experimental import pallas as pl
from jax.experimental.pallas import tpu as pltpu
from jax.sharding import PartitionSpec as P

PANEL = 512
PANELS = 2
INNER = 128
STRIP = 8
STEPS = PANEL // INNER
TICKS = 4
CHUNKS = 8
LAG = 3
EARLY = 5
HIGH = lax.Precision.HIGH


def dot(a, b, ca, cb, precision=HIGH):
    return lax.dot_general(
        a, b, (((ca,), (cb,)), ((), ())), precision=precision, preferred_element_type=jnp.float32
    )


def tree(terms):
    while len(terms) > 1:
        terms = [terms[i] + terms[i + 1] if i + 1 < len(terms) else terms[i] for i in range(0, len(terms), 2)]
    return terms[0]


def factor_corner(work, inv, tick):
    shape = (STRIP, INNER)
    n = INNER // STRIP
    sub = lax.broadcasted_iota(jnp.int32, shape, 0)
    lane = lax.broadcasted_iota(jnp.int32, shape, 1)

    def splat(x, t):
        return jnp.broadcast_to(x[t : t + 1, :], shape)

    def column(x, j):
        return jnp.broadcast_to(x[:, j : j + 1], shape)

    def block(a):
        return slice(a * STRIP, (a + 1) * STRIP)

    m = None
    for q in range(n):
        if m is None:
            m = [work[block(a), :] for a in range(n)]
        lo = q * STRIP
        panel = (lane >= lo) & (lane < lo + STRIP)
        rows = m[q]
        cols = [column(rows, lo + t) for t in range(STRIP)]
        full = jnp.where(panel, jnp.where(lane == lo + sub, 1.0, 0.0), rows)
        lower = full
        pivots = None
        for t in range(STRIP):
            pivot = splat(cols[t], t)
            pivots = pivot if pivots is None else jnp.where(sub >= t, pivot, pivots)
            scaled = cols[t] * (1.0 / pivot)
            both = jnp.where(sub == t, 0.0, scaled)
            for s in range(t + 1, STRIP):
                cols[s] = cols[s] - both * splat(cols[s], t)
            head = splat(full, t)
            full = full - both * head
            if t + 1 < STRIP:
                lower = lower - jnp.where(sub > t, scaled, 0.0) * head
        inv[block(q), :] = jnp.where(lane < lo + STRIP, lower * lax.rsqrt(pivots), 0.0)
        if q + 1 < n:
            full = full * (1.0 / pivots)
            heads = [splat(full, t) for t in range(STRIP)]
            for a in range(q + 1, n):
                parts = tree([column(m[a], lo + t) * heads[t] for t in range(STRIP)])
                m[a] = jnp.where(panel, 0.0, m[a]) - parts
        if (q + 1) % 4 == 0:
            if q + 1 < n:
                for a in range(q + 1, n):
                    work[block(a), :] = m[a]
                m = None
            tick((q + 1) // 4 - 1)


def factor_block(source, inverse, lower, work, inv, held, pivot_block, tick, first):
    def before(k):
        lo, hi = k * INNER, (k + 1) * INNER
        block = source[lo:hi, lo:hi]
        if k:
            row = dot(source[lo:hi, :lo], inverse[:lo, :lo], 1, 1)
            block = block - dot(row, row, 1, 1)
            held[:, :lo] = dot(row, inverse[:lo, :lo], 1, 0)
            if lower is not None:
                lower[lo:hi, :lo] = row
        work[...] = block
        pivot_block[...] = block

    def after(k):
        lo, hi = k * INNER, (k + 1) * INNER
        corner = inv[...]
        if k:
            inverse[lo:hi, :lo] = -dot(corner, held[:, :lo], 1, 0)
        inverse[lo:hi, lo:hi] = corner
        if lower is not None:
            lower[lo:hi, lo:hi] = dot(pivot_block[...], corner, 1, 1)
        if hi < PANEL:
            inverse[lo:hi, hi:] = jnp.zeros((INNER, PANEL - hi), jnp.float32)
            if lower is not None:
                lower[lo:hi, hi:] = jnp.zeros((INNER, PANEL - hi), jnp.float32)

    def step(k, carry):
        for static in range(STEPS):
            pl.when(k == static)(functools.partial(before, static))
        factor_corner(work, inv, lambda i: tick(k, i, first + TICKS * k + i))
        for static in range(STEPS):
            pl.when(k == static)(functools.partial(after, static))
        return carry

    lax.fori_loop(0, STEPS, step, 0)


def pick(index, table):
    value = 0
    for i, entry in enumerate(table):
        value = value + jnp.where(index == i, entry, 0)
    return value


def lead_kernel(
    groups, layer, s_ref, rowp, colp, inverse, lower, solved,
    theirs, diag, rest, work, inv, held, pivot_block,
    dsend, drecv, dlocal, asend, arecv, zsend, zrecv,
    bsend, brecv, bxsend, bxrecv, csend, crecv, cxsend, cxrecv, lsem,
):
    row_groups, col_groups = groups
    r, c, d = lax.axis_index("row"), lax.axis_index("col"), lax.axis_index("depth")
    ring = list(range(row_groups))
    if row_groups & (row_groups - 1) == 0:
        ring = [i ^ (i >> 1) for i in ring]
    place = [ring.index(i) for i in range(row_groups)]
    pos = pick(r, place)
    after = pick(r, [ring[(place[i] + 1) % row_groups] for i in range(row_groups)])
    before = pick(r, [ring[(place[i] - 1) % row_groups] for i in range(row_groups)])
    target = jnp.where(d == 0, after, before)
    half = PANEL // 2
    second = jnp.where(d == 0, 0, 1)

    def remote(src, dst, send, recv, device):
        return pltpu.make_async_remote_copy(
            src_ref=src, dst_ref=dst, send_sem=send, recv_sem=recv,
            device_id=device, device_id_type=pl.DeviceIdType.MESH,
        )

    def local(src, dst):
        copy = pltpu.make_async_copy(src, dst, lsem)
        copy.start()
        copy.wait()

    top = (r == 0) & (d == 0)
    origin0 = top & (c == 0)
    far = list(range(col_groups - 1, 0, -1))
    wide = list(range(row_groups - 1, 0, -1))

    def piece(ref, k):
        return ref.at[pl.ds(k * INNER, INNER), pl.ds(0, (k + 1) * INNER)]

    def direct(src, k, slot, device):
        return remote(piece(src, k), piece(diag, k), asend.at[k, slot], arecv.at[k], device)

    def planes(k, src, act):
        for i, other in enumerate(wide):
            act(direct(src, k, len(far) + i, {"row": other}))
        act(direct(src, k, len(far) + len(wide), {"depth": 1}))

    def launch(k):
        @pl.when(origin0)
        def _():
            for i, other in enumerate(far):
                direct(s_ref, k, i, {"col": other}).start()
            planes(k, s_ref, lambda copy: copy.start())
            local(piece(s_ref, k), piece(diag, k))

    def arrive(k):
        @pl.when(jnp.logical_not(origin0))
        def _():
            direct(diag, k, 0, {"depth": 1 - d}).wait_recv()

        @pl.when(top & (c > 0))
        def _():
            planes(k, diag, lambda copy: copy.start())

        @pl.when((r > 0) & (d == 0))
        def _():
            direct(diag, k, len(far) + len(wide), {"depth": 1}).start()

    def settle(k):
        @pl.when(origin0)
        def _():
            for i, other in enumerate(far):
                direct(s_ref, k, i, {"col": other}).wait_send()

        @pl.when(top)
        def _():
            planes(k, diag, lambda copy: copy.wait_send())

        @pl.when((r > 0) & (d == 0))
        def _():
            direct(diag, k, len(far) + len(wide), {"depth": 1}).wait_send()

    def line(p, k, way):
        size = PANEL // CHUNKS
        block = rowp.at[p, pl.ds(pl.multiple_of(k * size, size), size)]
        return remote(block, block, zsend.at[p, k, max(way, 0)], zrecv.at[p, k], {"col": c + way})

    def line_set(p):
        hop = jnp.where(c > p, c - p, p - c)
        up, down = (c >= p) & (c < col_groups - 1), (c <= p) & (c > 0)
        needed = jnp.logical_not((r == 0) & (d == 0)) if p == 0 else jnp.bool_(True)
        return hop, up, down, needed

    def stream(dst, size, root, sems, index, k):
        send, recv, xsend, xrecv = sems
        rel = jnp.where(d == 0, (pos - place[root] + row_groups) % row_groups, (place[root] - pos + row_groups) % row_groups)
        own, other = size

        def hop():
            block = dst.at[own]
            return remote(block, block, send.at[index, k], recv.at[index, k], {"row": target})

        def across(kind):
            block = dst.at[(own, other)[kind]]
            return remote(block, block, xsend.at[index, kind, k], xrecv.at[index, kind, k], {"depth": 1 - d})

        return rel, hop, across

    def inject(src, dst, size, root, sems, index, k):
        rel, hop, across = stream(dst, size, root, sems, index, k)
        own, other = size
        local(src.at[other], dst.at[other])
        across(1).start()
        local(src.at[own], dst.at[own])
        hop().start()
        across(0).start()

    def relay(dst, size, root, sems, index, k):
        rel, hop, across = stream(dst, size, root, sems, index, k)

        @pl.when(rel == 0)
        def _():
            across(1).wait_recv()

        @pl.when(rel > 0)
        def _():
            hop().wait_recv()

        @pl.when(rel < row_groups - 1)
        def _():
            hop().start()

        @pl.when(rel > 0)
        def _():
            across(0).start()

    def finish(dst, size, root, sems, index, k, arrived):
        rel, hop, across = stream(dst, size, root, sems, index, k)
        origin = (rel == 0) & (d == 0)
        if arrived:
            @pl.when(jnp.logical_not(origin))
            def _():
                across(0).wait_recv()
            return

        @pl.when(origin)
        def _():
            across(1).wait_send()

        @pl.when((rel > 0) | origin)
        def _():
            across(0).wait_send()

        @pl.when(rel < row_groups - 1)
        def _():
            hop().wait_send()

    bsems = (bsend, brecv, bxsend, bxrecv)
    csems = (csend, crecv, cxsend, cxrecv)

    def bsize(k):
        size = PANEL // CHUNKS // 2
        return (
            pl.ds(pl.multiple_of((2 * k + d) * size, size), size),
            pl.ds(pl.multiple_of((2 * k + 1 - d) * size, size), size),
        )

    def csize(k):
        size = half // CHUNKS
        return (
            pl.ds(pl.multiple_of(d * half + k * size, size), size),
            pl.ds(pl.multiple_of((1 - d) * half + k * size, size), size),
        )

    last = PANELS - 1
    blocks_args = lambda item, k: (rest.at[item], bsize(k), item, bsems, item, k)
    cols_args = lambda p, k: (colp.at[p], csize(k), p, csems, p, k)

    def tick(n):
        for p in reversed(range(PANELS)):
            hop, up, down, needed = line_set(p)
            k = n - (CHUNKS * (last - p) + CHUNKS * PANELS * d + LAG * hop)

            @pl.when((k >= 0) & (k < CHUNKS) & needed)
            def _():
                @pl.when(c == p)
                def _():
                    size = PANEL // CHUNKS
                    rows = pl.ds(pl.multiple_of(k * size, size), size)
                    local(s_ref.at[rows, pl.ds(0, PANEL)], rowp.at[p, rows])

                @pl.when(c != p)
                def _():
                    line(p, k, 1).wait_recv()

                @pl.when(up)
                def _():
                    line(p, k, 1).start()

                @pl.when(down)
                def _():
                    line(p, k, -1).start()

                if p == last:
                    for item in range(PANELS):
                        @pl.when((r == item) & (d == 0))
                        def _():
                            inject(rowp.at[last], *blocks_args(item, k))

        hop = jnp.where(c > last, c - last, last - c)
        for item in range(PANELS):
            rel = stream(*blocks_args(item, 0))[0]
            k = n - (LAG * hop + LAG * rel + second)

            @pl.when((k >= 0) & (k < CHUNKS) & ((rel > 0) | (d != 0)))
            def _():
                relay(*blocks_args(item, k))

        for p in range(PANELS):
            rel = stream(*cols_args(p, 0))[0]
            k = n - (CHUNKS * p + CHUNKS + 4 + LAG * rel + second)

            @pl.when((k >= 0) & (k < CHUNKS))
            def _():
                @pl.when((rel == 0) & (d == 0))
                def _():
                    inject(s_ref, *cols_args(p, k))

                @pl.when((rel > 0) | (d != 0))
                def _():
                    relay(*cols_args(p, k))

    def ticks(lo, hi):
        def step(n, carry):
            tick(n)
            return carry

        lax.fori_loop(lo, hi, step, 0)

    def exchange(k):
        rows = pl.ds(k * INNER, INNER)
        mine = layer.at[0, pl.ds(pl.multiple_of(d * PANEL + k * INNER, INNER), INNER)]
        other = layer.at[0, pl.ds(pl.multiple_of((1 - d) * PANEL + k * INNER, INNER), INNER)]
        copy = remote(other, theirs.at[rows], dsend.at[k], drecv.at[k], {"depth": 1 - d})
        return copy, pltpu.make_async_copy(mine, s_ref.at[rows], dlocal.at[k])

    for k in range(STEPS):
        for copy in exchange(k):
            copy.start()
    for k in range(STEPS):
        copy, mine = exchange(k)
        mine.wait()
        copy.wait_recv()

        def add(i, carry):
            rows = pl.ds(pl.multiple_of(k * INNER + i * 32, 32), 32)
            s_ref[rows, :] = s_ref[rows, :] + theirs[rows, :]
            return carry

        lax.fori_loop(0, INNER // 32, add, 0)
        launch(k)

    @pl.when(top)
    def _():
        arrive(0)

    ticks(0, EARLY)

    @pl.when(jnp.logical_not(top))
    def _():
        arrive(0)

    def side(k, i, n):
        tick(n)
        if i == 2:
            for static in range(STEPS - 1):
                @pl.when(k == static)
                def _():
                    arrive(static + 1)

    scratch = (work, inv, held, pivot_block)
    factor_block(diag, inverse.at[0], lower, *scratch, side, EARLY)
    base = EARLY + TICKS * STEPS
    reach = CHUNKS + LAG * max(last, col_groups - 1 - last) + LAG * (row_groups - 1) + 1
    resume = max(base, reach)
    ticks(base, resume)

    def landed(k, carry):
        for item in range(PANELS):
            finish(*blocks_args(item, k), True)
        return carry

    lax.fori_loop(0, CHUNKS, landed, 0)
    solved[...] = dot(inverse[0], rest[0], 1, 0)
    whole = theirs.at[:, pl.ds(0, PANEL)]
    whole[...] = rest[1] - dot(solved[...], solved[...], 0, 0)
    factor_block(whole, inverse.at[1], None, *scratch, lambda k, i, n: tick(n), resume)
    lines = 2 * PANELS * CHUNKS + LAG * max(col_groups - 1, last)
    rings = PANELS * CHUNKS + CHUNKS + 5 + LAG * (row_groups - 1)
    ticks(resume + TICKS * STEPS, max(lines, rings))

    def close(k, carry):
        for p in range(PANELS):
            hop, up, down, needed = line_set(p)
            for way, on in ((1, up), (-1, down)):
                @pl.when(on & needed)
                def _():
                    line(p, k, way).wait_send()
            finish(*blocks_args(p, k), False)
            finish(*cols_args(p, k), True)
            finish(*cols_args(p, k), False)
        return carry

    lax.fori_loop(0, CHUNKS, close, 0)
    for k in range(STEPS):
        settle(k)
        exchange(k)[0].wait_send()


def lead(layer, row_groups, col_groups):
    cols = layer.shape[2]
    dma = pltpu.SemaphoreType.DMA
    vmem = pl.BlockSpec(memory_space=pltpu.VMEM)
    f32 = lambda *shape: jax.ShapeDtypeStruct(shape, jnp.float32)
    buffer = lambda *shape: pltpu.VMEM(shape, jnp.float32)
    return pl.pallas_call(
        functools.partial(lead_kernel, (row_groups, col_groups)),
        out_shape=(
            f32(PANEL, cols),
            f32(PANELS, PANEL, PANEL),
            f32(PANELS, PANEL, cols),
            f32(PANELS, PANEL, PANEL),
            f32(PANEL, PANEL),
            f32(PANEL, PANEL),
        ),
        in_specs=[pl.BlockSpec(memory_space=pl.ANY)],
        out_specs=(vmem,) * 6,
        scratch_shapes=[
            buffer(PANEL, cols),
            buffer(PANEL, PANEL),
            buffer(PANELS, PANEL, PANEL),
            buffer(INNER, INNER),
            buffer(INNER, INNER),
            buffer(INNER, PANEL),
            buffer(INNER, INNER),
            dma((STEPS,)),
            dma((STEPS,)),
            dma((STEPS,)),
            dma((STEPS, row_groups + col_groups - 1)),
            dma((STEPS,)),
            dma((PANELS, CHUNKS, 2)),
            dma((PANELS, CHUNKS)),
        ]
        + 2 * [dma((PANELS, CHUNKS)), dma((PANELS, CHUNKS)), dma((PANELS, 2, CHUNKS)), dma((PANELS, 2, CHUNKS))]
        + [dma],
        compiler_params=pltpu.CompilerParams(has_side_effects=True, vmem_limit_bytes=60 * 1024 * 1024),
        name="lead",
    )(layer)


def per_device(layers):
    row_groups = lax.axis_size("row")
    col_groups = lax.axis_size("col")
    depth_groups = lax.axis_size("depth")
    row = lax.axis_index("row")
    col = lax.axis_index("col")
    depth = lax.axis_index("depth")
    cols_local = layers.shape[2]
    assert layers.shape[1] == PANEL * depth_groups and depth_groups == 2
    assert PANELS == 2 and row_groups >= PANELS and col_groups >= PANELS

    swap = [(0, 1), (1, 0)]
    own_block = row + row_groups * depth
    col_block = jnp.arange(cols_local, dtype=jnp.int32) // PANEL * col_groups + col

    summed, rowp, colp, inverse, lower, solved = lead(layers, row_groups, col_groups)
    rows = [rowp[p] for p in range(PANELS)]
    cols = [colp[p] for p in range(PANELS)]
    factors, left, right = [], [], []
    for p in range(PANELS):
        c_rows = jnp.where(own_block >= p, dot(rows[p], inverse[p], 1, 1), 0.0)
        if p == 0:
            c_rows = jnp.where(own_block == 0, lower, c_rows)
        below = jnp.where(own_block > p, c_rows, 0.0)
        c_cols = dot(inverse[p], cols[p], 1, 0)
        c_cols = jnp.where((col_block > p)[None, :], c_cols, 0.0)
        factors.append(c_rows)
        left.append(below)
        right.append(c_cols)
        for q in range(p + 1, PANELS):
            rows[q] = rows[q] - dot(below, solved, 1, 0)
            cols[q] = cols[q] - dot(solved, c_cols, 0, 0)
    update = dot(jnp.concatenate(left, 1), jnp.concatenate(right, 0), 1, 0)
    schur = summed - update
    factor = jnp.stack(factors)
    width = PANEL // depth_groups
    kept = lax.dynamic_slice_in_dim(factor, depth * width, width, 2)
    sent = lax.dynamic_slice_in_dim(factor, (1 - depth) * width, width, 2)
    got = lax.ppermute(sent, "depth", swap)
    first = jnp.where(depth == 0, kept, got)
    second = jnp.where(depth == 0, got, kept)
    return jnp.concatenate([first, second], axis=1), schur


def solution(mesh):
    return jax.shard_map(
        per_device,
        mesh=mesh,
        in_specs=(P("depth", "row", "col"),),
        out_specs=(P(None, "row", "depth"), P(("row", "depth"), "col")),
        check_vma=False,
    )
```

time: 186 us -> 130 us (0.70)
  the two profiles are of different devices: /device:TPU:28 before, /device:TPU:25 now
where the time goes in v2:
time: 130 us
  Pallas kernels  103 us (79%)
  matrix products  18.7 us (14%)
  other arithmetic  4.02 us (3%)
  starting transfers between devices  2.93 us (2%)
    pallas_call x1, Pallas kernels, lead(): pl.pallas_call(functools.partial(lead_kernel, (row_groups, col_groups)),...  103 us
    dot_general x7, matrix products, dot(): lax.dot_general(a, b, (((ca,), (cb,)), ((), ())), precision=precision, pr...  18.7 us
    ppermute x1, starting transfers between devices, per_device(): got = lax.ppermute(sent, 'depth', swap)  2.93 us
  transfers between devices with their start and end apart: 1, of which 0 were waited for; matrix products, arithmetic and copies ran while one was open for 10% of the time, Pallas kernels for 0%

profile of v2, /device:TPU:25, one launch (start us, length us, event | category | flops | bytes accessed | tf_op | source)
XLA Modules:
  0.0 130.2 jit_solution(9817206509884473683)
XLA Ops:
  0.6 103.2 %lead.1 = (f32[512,1024]{1,0:T(8,128)}, f32[2,512,512]{2,1,0:T(8,128)}, f32[2,512,1024]{2,1,0:T(8,128)}, f32[2,512,512]{2,1,0:T(8,128)}, f32[512,512]{1,0:T(8,128)}, /*index=5*/f32[512,512]{1,0:T(8,128)}) custom-call(f32[1,1024,1024]{2,1,0:T(8,128)} %layer.1), custom_call_target="tpu_custom_call" | custom-call | tf_op jit(solution)/shard_map/lead/pallas_call | solution.py:454
  103.8 0.0 copy-start.3
  103.8 0.0 copy-start.7
  103.8 2.7 %broadcast_select_fusion.1 = (f32[512,512]{1,0:T(8,128)S(1)}, f32[512,512]{1,0:T(8,128)S(1)}) fusion(pred[]{:T(512)S(6)} %gt.22, f32[512,512]{1,0:T(8,128)} %get-tuple-element.8, f32[2,512,512]{2,1,0:T(8,128)} %get-tuple-element.10, f32[2,512,512]{2,1,0:T(8,128)} %get-tuple-element.9, pred[]{:T(512)S(6)} %ge.6, pred[]{:T(512)S(6)} %eq.8), kind=kOutput, calls=%fused_computation.39 | convolution fusion | flops 806092800 | bytes 5242883 | tf_op jit(solution)/shard_map/dot_general | solution.py:23
  106.6 0.0 copy-done.3
  106.6 0.0 copy-done.7
  106.6 0.0 copy-start
  106.6 1.0 convolution_subtract_fusion
  107.7 0.5 copy-done
  108.2 2.0 %broadcast_select_fusion = (f32[512,512]{1,0:T(8,128)}, f32[512,512]{1,0:T(8,128)S(1)}) fusion(pred[]{:T(512)S(6)} %gt.23, f32[512,512]{1,0:T(8,128)S(1)} %convolution_subtract_fusion, f32[2,512,512]{2,1,0:T(8,128)S(1)} %copy-done, pred[]{:T(512)S(6)} %ge.7), kind=kOutput, calls=%fused_computation.38 | convolution fusion | flops 805830656 | bytes 4194306 | tf_op jit(solution)/shard_map/dot_general | solution.py:23
  110.2 1.1 fusion.17
  111.3 2.9 %collective-permute-start = (f32[2,512,256]{2,1,0:T(8,128)}, f32[2,512,256]{2,1,0:T(8,128)}, u32[]{:S(2)}, u32[]{:S(2)}) collective-permute-start(f32[2,512,256]{2,1,0:T(8,128)} %fusion.17), channel_id=1, source_target_pairs={{0,1},{1,0},{2,3},{3,2},{4,5},{5,4},{6,7},{7,6},{8,9},{9,8},{10,11... | collective-permute-start | bytes 3145736 | tf_op jit(solution)/shard_map/ppermute | solution.py:527
  114.2 0.0 copy-start.4
  114.2 0.0 copy-start.5
  114.2 3.9 %fusion.13 = f32[512,1024]{1,0:T(8,128)S(1)} fusion(f32[2,512,1024]{2,1,0:T(8,128)} %get-tuple-element.13, pred[1024]{0:T(1024)(128)(4,1)S(1)} %get-tuple-element.21, f32[2,512,512]{2,1,0:T(8,128)} %get-tuple-element.10), kind=kOutput, calls=%fused_computation.20 | convolution fusion | flops 1611137024 | bytes 5243904 | tf_op jit(solution)/shard_map/dot_general | solution.py:23
  118.2 0.0 copy-done.4
  118.2 0.0 copy-start.1
  118.2 1.9 %fusion.42 = f32[1024,512]{0,1:T(8,128)S(1)} fusion(f32[512,1024]{1,0:T(8,128)S(1)} %fusion.13, f32[512,512]{1,0:T(8,128)S(1)} %copy-done.4), kind=kOutput, calls=%fused_computation.54 | convolution fusion | flops 1610612736 | bytes 5242880 | tf_op jit(solution)/shard_map/dot_general | solution.py:23
  120.1 0.0 copy-done.5
  120.1 0.0 copy-done.1
  120.1 0.0 copy-start.2
  120.1 0.0 copy-start.6
  120.1 1.9 %select_bitcast_fusion = f32[512,1024]{1,0:T(8,128)S(1)} fusion(f32[1024,512]{0,1:T(8,128)S(1)} %fusion.42, f32[2,512,1024]{2,1,0:T(8,128)S(1)} %copy-done.5, pred[1024]{0:T(1024)(128)(4,1)S(1)} %get-tuple-element.20, f32[2,512,512]{2,1,0:T(8,128)S(1)} %copy-done.1), kind=kOutput, calls=%fused_computation.17 | convolution fusion | flops 1611661312 | bytes 7341056 | tf_op jit(solution)/shard_map/dot_general | solution.py:23
  122.0 0.0 copy-done.2
  122.0 0.0 copy-done.6
  122.1 5.2 %fusion.25 = f32[512,1024]{1,0:T(8,128)} fusion(f32[512,1024]{1,0:T(8,128)S(1)} %copy-done.6, f32[512,1024]{1,0:T(8,128)S(1)} %select_bitcast_fusion, f32[512,1024]{1,0:T(8,128)S(1)} %fusion.13, f32[512,512]{1,0:T(8,128)S(1)} %copy-done.2, f32[512,512]{1,0:T(8,128)S(1)} %get-tuple-element.16), kind=kOutput, calls=%fused_computation.33 | convolution fusion | flops 3223322624 | bytes 10485760 | tf_op jit(solution)/shard_map/dot_general | solution.py:23
  127.2 0.0 collective-permute-done
  127.2 1.5 %broadcast_select_fusion.3 = (f32[2,512,256]{2,1,0:T(8,128)S(1)}, f32[2,512,256]{2,1,0:T(8,128)S(1)}) fusion(f32[2,512,256]{2,1,0:T(8,128)} %collective-permute-done, pred[]{:T(512)S(6)} %eq.7, s32[]{:T(128)S(6)} %select_n.83, f32[1,512,512]{2,1,0:T(8,128)S(1)} %bitcast.48, f32[1,512,512]{2,1,0:T(8,128)S(1)} %bitcast.50), kind=kLoop, calls=%fused_computation.41 | loop fusion | flops 1048576 | bytes 5242885 | tf_op jit(solution)/shard_map/jit(_where)/select_n | solution.py:528
  128.7 1.5 %pad_maximum_fusion = f32[2,1024,256]{2,1,0:T(8,128)} fusion(f32[2,512,256]{2,1,0:T(8,128)S(1)} %get-tuple-element.15, f32[2,512,256]{2,1,0:T(8,128)S(1)} %get-tuple-element.14), kind=kLoop, calls=%fused_computation.8 | loop fusion | flops 524288 | bytes 4194304 | tf_op jit(solution)/shard_map/concatenate | solution.py:530
  (1 shorter events, 0.0 us)
Async XLA Ops:
  103.8 2.8 %copy-start.3 = (f32[512,512]{1,0:T(8,128)S(1)}, f32[512,512]{1,0:T(8,128)}, u32[]{:S(2)}) copy-start(f32[512,512]{1,0:T(8,128)} %get-tuple-element.11) | copy-start | bytes 3145732
  103.8 2.8 %copy-start.7 = (f32[2,512,512]{2,1,0:T(8,128)S(1)}, f32[2,512,512]{2,1,0:T(8,128)}, u32[]{:S(2)}) copy-start(f32[2,512,512]{2,1,0:T(8,128)} %get-tuple-element.9) | copy-start | bytes 6291460
  106.6 1.6 %copy-start = (f32[2,512,512]{2,1,0:T(8,128)S(1)}, f32[2,512,512]{2,1,0:T(8,128)}, u32[]{:S(2)}) copy-start(f32[2,512,512]{2,1,0:T(8,128)} %get-tuple-element.10) | copy-start | bytes 6291460
  111.3 15.9 %collective-permute-start = (f32[2,512,256]{2,1,0:T(8,128)}, f32[2,512,256]{2,1,0:T(8,128)}, u32[]{:S(2)}, u32[]{:S(2)}) collective-permute-start(f32[2,512,256]{2,1,0:T(8,128)} %fusion.17), channel_id=1, source_target_pairs={{0,1},{1,0},{2,3},{3,2},{4,5},{5,4},{6,7},{7,6},{8,9},{9,8},{10,11... | collective-permute-start | bytes 3145736 | tf_op jit(solution)/shard_map/ppermute | solution.py:527
  114.2 3.9 %copy-start.4 = (f32[512,512]{1,0:T(8,128)S(1)}, f32[512,512]{1,0:T(8,128)}, u32[]{:S(2)}) copy-start(f32[512,512]{1,0:T(8,128)} %get-tuple-element.11) | copy-start | bytes 3145732
  114.2 5.9 %copy-start.5 = (f32[2,512,1024]{2,1,0:T(8,128)S(1)}, f32[2,512,1024]{2,1,0:T(8,128)}, u32[]{:S(2)}) copy-start(f32[2,512,1024]{2,1,0:T(8,128)} %get-tuple-element.13) | copy-start | bytes 12582916
  118.2 1.9 %copy-start.1 = (f32[2,512,512]{2,1,0:T(8,128)S(1)}, f32[2,512,512]{2,1,0:T(8,128)}, u32[]{:S(2)}) copy-start(f32[2,512,512]{2,1,0:T(8,128)} %get-tuple-element.10) | copy-start | bytes 6291460
  120.1 1.9 %copy-start.2 = (f32[512,512]{1,0:T(8,128)S(1)}, f32[512,512]{1,0:T(8,128)}, u32[]{:S(2)}) copy-start(f32[512,512]{1,0:T(8,128)} %get-tuple-element.18) | copy-start | bytes 3145732
  120.1 1.9 %copy-start.6 = (f32[512,1024]{1,0:T(8,128)S(1)}, f32[512,1024]{1,0:T(8,128)}, u32[]{:S(2)}) copy-start(f32[512,1024]{1,0:T(8,128)} %get-tuple-element.12) | copy-start | bytes 6291460

commit v3 on v2

--- a/solution.py
+++ b/solution.py
@@ -15,7 +15,9 @@
 TICKS = 4
 CHUNKS = 8
 LAG = 3
-EARLY = 5
+SLACK = 4
+START = 8
+EARLY = 7
 HIGH = lax.Precision.HIGH
 
 
@@ -83,7 +85,7 @@
             tick((q + 1) // 4 - 1)
 
 
-def factor_block(source, inverse, lower, work, inv, held, pivot_block, tick, first):
+def factor_block(source, inverse, lower, work, inv, held, pivot_block, tick, first, extra=None):
     def before(k):
         lo, hi = k * INNER, (k + 1) * INNER
         block = source[lo:hi, lo:hi]
@@ -115,6 +117,8 @@
         factor_corner(work, inv, lambda i: tick(k, i, first + TICKS * k + i))
         for static in range(STEPS):
             pl.when(k == static)(functools.partial(after, static))
+        if extra is not None:
+            pl.when(k == extra[0])(extra[1])
         return carry
 
     lax.fori_loop(0, STEPS, step, 0)
@@ -128,10 +132,10 @@
 
 
 def lead_kernel(
-    groups, layer, s_ref, rowp, colp, inverse, lower, solved,
-    theirs, diag, rest, work, inv, held, pivot_block,
+    groups, layer, s_ref, factor, left, ccols,
+    rowp, colp, inverse, lower, solved, crow, theirs, diag, rest, work, inv, held, pivot_block,
     dsend, drecv, dlocal, asend, arecv, zsend, zrecv,
-    bsend, brecv, bxsend, bxrecv, csend, crecv, cxsend, cxrecv, lsem,
+    bsend, brecv, bxsend, bxrecv, csend, crecv, cxsend, cxrecv, fsend, frecv, lsem,
 ):
     row_groups, col_groups = groups
     r, c, d = lax.axis_index("row"), lax.axis_index("col"), lax.axis_index("depth")
@@ -144,6 +148,7 @@
     before = pick(r, [ring[(place[i] - 1) % row_groups] for i in range(row_groups)])
     target = jnp.where(d == 0, after, before)
     half = PANEL // 2
+    last = PANELS - 1
     second = jnp.where(d == 0, 0, 1)
 
     def remote(src, dst, send, recv, device):
@@ -159,7 +164,8 @@
 
     top = (r == 0) & (d == 0)
     origin0 = top & (c == 0)
-    far = list(range(col_groups - 1, 0, -1))
+    far = list(range(max(col_groups - 2, 1), 0, -1))
+    relays = top & (c == col_groups - 2) if col_groups > 2 else jnp.bool_(False)
     wide = list(range(row_groups - 1, 0, -1))
 
     def piece(ref, k):
@@ -186,6 +192,10 @@
         def _():
             direct(diag, k, 0, {"depth": 1 - d}).wait_recv()
 
+        @pl.when(relays)
+        def _():
+            direct(diag, k, 0, {"col": c + 1}).start()
+
         @pl.when(top & (c > 0))
         def _():
             planes(k, diag, lambda copy: copy.start())
@@ -199,6 +209,10 @@
         def _():
             for i, other in enumerate(far):
                 direct(s_ref, k, i, {"col": other}).wait_send()
+
+        @pl.when(relays)
+        def _():
+            direct(diag, k, 0, {"col": c + 1}).wait_send()
 
         @pl.when(top)
         def _():
@@ -216,8 +230,15 @@
     def line_set(p):
         hop = jnp.where(c > p, c - p, p - c)
         up, down = (c >= p) & (c < col_groups - 1), (c <= p) & (c > 0)
-        needed = jnp.logical_not((r == 0) & (d == 0)) if p == 0 else jnp.bool_(True)
-        return hop, up, down, needed
+        lead = r < PANELS
+        first = lead & (d == 0)
+        stride = jnp.where(lead, 1, 2)
+        begin = jnp.where(lead, CHUNKS * (1 + p), 2 * CHUNKS * p) + SLACK * hop
+        needed = jnp.logical_not(first)
+        if p == last:
+            begin = jnp.where(first, LAG * hop, begin)
+            needed = jnp.bool_(True)
+        return begin, stride, up, down, needed
 
     def stream(dst, size, root, sems, index, k):
         send, recv, xsend, xrecv = sems
@@ -300,16 +321,15 @@
             pl.ds(pl.multiple_of((1 - d) * half + k * size, size), size),
         )
 
-    last = PANELS - 1
     blocks_args = lambda item, k: (rest.at[item], bsize(k), item, bsems, item, k)
     cols_args = lambda p, k: (colp.at[p], csize(k), p, csems, p, k)
 
     def tick(n):
         for p in reversed(range(PANELS)):
-            hop, up, down, needed = line_set(p)
-            k = n - (CHUNKS * (last - p) + CHUNKS * PANELS * d + LAG * hop)
-
-            @pl.when((k >= 0) & (k < CHUNKS) & needed)
+            begin, stride, up, down, needed = line_set(p)
+            k = (n - begin) // stride
+
+            @pl.when((n >= begin) & ((n - begin) % stride == 0) & (k < CHUNKS) & needed)
             def _():
                 @pl.when(c == p)
                 def _():
@@ -346,7 +366,7 @@
 
         for p in range(PANELS):
             rel = stream(*cols_args(p, 0))[0]
-            k = n - (CHUNKS * p + CHUNKS + 4 + LAG * rel + second)
+            k = n - (START + CHUNKS * p + SLACK * rel + second)
 
             @pl.when((k >= 0) & (k < CHUNKS))
             def _():
@@ -398,13 +418,16 @@
     def _():
         arrive(0)
 
+    other = jnp.logical_not(top)
+    plan = [(0, 1, top), (2, 2, top), (6, 3, top), (2, 1, other), (6, 2, other), (10, 3, other)]
+
     def side(k, i, n):
         tick(n)
-        if i == 2:
-            for static in range(STEPS - 1):
-                @pl.when(k == static)
-                def _():
-                    arrive(static + 1)
+        for at, piece_index, who in plan:
+            if i == at % TICKS:
+                @pl.when((k == at // TICKS) & who)
+                def _():
+                    arrive(piece_index)
 
     scratch = (work, inv, held, pivot_block)
     factor_block(diag, inverse.at[0], lower, *scratch, side, EARLY)
@@ -420,29 +443,106 @@
 
     lax.fori_loop(0, CHUNKS, landed, 0)
     solved[...] = dot(inverse[0], rest[0], 1, 0)
+
+    @pl.when((r == 1) & (d == 0))
+    def _():
+        lower[...] = solved[...].T
+
     whole = theirs.at[:, pl.ds(0, PANEL)]
     whole[...] = rest[1] - dot(solved[...], solved[...], 0, 0)
-    factor_block(whole, inverse.at[1], None, *scratch, lambda k, i, n: tick(n), resume)
-    lines = 2 * PANELS * CHUNKS + LAG * max(col_groups - 1, last)
-    rings = PANELS * CHUNKS + CHUNKS + 5 + LAG * (row_groups - 1)
-    ticks(resume + TICKS * STEPS, max(lines, rings))
-
-    def close(k, carry):
-        for p in range(PANELS):
-            hop, up, down, needed = line_set(p)
-            for way, on in ((1, up), (-1, down)):
-                @pl.when(on & needed)
-                def _():
-                    line(p, k, way).wait_send()
-            finish(*blocks_args(p, k), False)
-            finish(*cols_args(p, k), True)
-            finish(*cols_args(p, k), False)
-        return carry
-
-    lax.fori_loop(0, CHUNKS, close, 0)
     for k in range(STEPS):
         settle(k)
         exchange(k)[0].wait_send()
+
+    own_block = r + row_groups * d
+
+    def tiles(count, size, body):
+        def step(t, carry):
+            body(pl.ds(pl.multiple_of(t * size, size), size), t)
+            return carry
+
+        lax.fori_loop(0, count // size, step, 0)
+
+    def live(t, p):
+        return t * col_groups + c > p
+
+    def first_rows(lanes, t):
+        value = jnp.where(own_block < PANELS, lower[:, lanes], dot(rowp[0], inverse[0, lanes, :], 1, 1))
+        crow[0, :, lanes] = value
+        left[:, lanes] = jnp.where(own_block > 0, value, 0.0)
+
+    def first_cols(lanes, t):
+        value = jnp.where(live(t, 0), dot(inverse[0], colp[0, :, lanes], 1, 0), 0.0)
+        ccols[:, lanes] = value
+        s_ref[:, lanes] = s_ref[:, lanes] - dot(left[...], value, 1, 0)
+
+    def between_rows(lanes, t):
+        rowp[1, :, lanes] = rowp[1, :, lanes] - dot(left[...], solved[:, lanes], 1, 0)
+
+    def second_rows(lanes, t):
+        value = jnp.where(own_block > 0, dot(rowp[1], inverse[1, lanes, :], 1, 1), 0.0)
+        crow[1, :, lanes] = value
+        left[:, lanes] = jnp.where(own_block > 1, value, 0.0)
+
+    def second_cols(lanes, t):
+        value = colp[1, :, lanes] - dot(solved[...], ccols[:, lanes], 0, 0)
+        value = dot(inverse[1], value, 1, 0)
+        value = jnp.where(live(t, 1), value, 0.0)
+        s_ref[:, lanes] = s_ref[:, lanes] - dot(left[...], value, 1, 0)
+
+    def arrived_cols(p):
+        def step(k, carry):
+            finish(*cols_args(p, k), True)
+            return carry
+
+        lax.fori_loop(0, CHUNKS, step, 0)
+
+    def give(p):
+        sent = crow.at[p, :, pl.ds(pl.multiple_of((1 - d) * half, half), half)]
+        there = factor.at[p, pl.ds(pl.multiple_of(d * PANEL, PANEL), PANEL), :]
+        return remote(sent, there, fsend.at[p], frecv.at[p], {"depth": 1 - d})
+
+    def keep(p):
+        kept = crow[p, :, pl.ds(pl.multiple_of(d * half, half), half)]
+        factor[p, pl.ds(pl.multiple_of(d * PANEL, PANEL), PANEL), :] = kept
+
+    def first_panel():
+        tiles(PANEL, half, first_rows)
+        arrived_cols(0)
+        tiles(s_ref.shape[1], PANEL, first_cols)
+        keep(0)
+        give(0).start()
+
+    lines = 2 * PANELS * CHUNKS + SLACK * max(col_groups - 1, last)
+    rings = PANELS * CHUNKS + START + 1 + SLACK * (row_groups - 1)
+    ready = max(lines - CHUNKS * PANELS, rings - CHUNKS, 2 * CHUNKS * PANELS)
+    early = -(-(ready - resume) // TICKS) - 1
+    extra = (early, first_panel) if early < STEPS else None
+    factor_block(whole, inverse.at[1], None, *scratch, lambda k, i, n: tick(n), resume, extra)
+    ticks(resume + TICKS * STEPS, max(lines, rings))
+    if extra is None:
+        first_panel()
+
+    def close(k, carry):
+        for p in range(PANELS):
+            begin, stride, up, down, needed = line_set(p)
+            for way, on in ((1, up), (-1, down)):
+                @pl.when(on & needed)
+                def _():
+                    line(p, k, way).wait_send()
+            finish(*blocks_args(p, k), False)
+            finish(*cols_args(p, k), False)
+        return carry
+
+    lax.fori_loop(0, CHUNKS, close, 0)
+    arrived_cols(1)
+    tiles(PANEL, half, between_rows)
+    tiles(PANEL, half, second_rows)
+    keep(1)
+    give(1).start()
+    tiles(s_ref.shape[1], PANEL, second_cols)
+    for p in range(PANELS):
+        give(p).wait()
 
 
 def lead(layer, row_groups, col_groups):
@@ -455,15 +555,19 @@
         functools.partial(lead_kernel, (row_groups, col_groups)),
         out_shape=(
             f32(PANEL, cols),
-            f32(PANELS, PANEL, PANEL),
-            f32(PANELS, PANEL, cols),
-            f32(PANELS, PANEL, PANEL),
-            f32(PANEL, PANEL),
-            f32(PANEL, PANEL),
+            f32(PANELS, 2 * PANEL, PANEL // 2),
         ),
         in_specs=[pl.BlockSpec(memory_space=pl.ANY)],
-        out_specs=(vmem,) * 6,
+        out_specs=(vmem,) * 2,
         scratch_shapes=[
+            buffer(PANEL, PANEL),
+            buffer(PANEL, cols),
+            buffer(PANELS, PANEL, PANEL),
+            buffer(PANELS, PANEL, cols),
+            buffer(PANELS, PANEL, PANEL),
+            buffer(PANEL, PANEL),
+            buffer(PANEL, PANEL),
+            buffer(PANELS, PANEL, PANEL),
             buffer(PANEL, cols),
             buffer(PANEL, PANEL),
             buffer(PANELS, PANEL, PANEL),
@@ -480,7 +584,7 @@
             dma((PANELS, CHUNKS)),
         ]
         + 2 * [dma((PANELS, CHUNKS)), dma((PANELS, CHUNKS)), dma((PANELS, 2, CHUNKS)), dma((PANELS, 2, CHUNKS))]
-        + [dma],
+        + [dma((PANELS,)), dma((PANELS,)), dma],
         compiler_params=pltpu.CompilerParams(has_side_effects=True, vmem_limit_bytes=60 * 1024 * 1024),
         name="lead",
     )(layer)
@@ -490,44 +594,11 @@
     row_groups = lax.axis_size("row")
     col_groups = lax.axis_size("col")
     depth_groups = lax.axis_size("depth")
-    row = lax.axis_index("row")
-    col = lax.axis_index("col")
-    depth = lax.axis_index("depth")
-    cols_local = layers.shape[2]
     assert layers.shape[1] == PANEL * depth_groups and depth_groups == 2
     assert PANELS == 2 and row_groups >= PANELS and col_groups >= PANELS
 
-    swap = [(0, 1), (1, 0)]
-    own_block = row + row_groups * depth
-    col_block = jnp.arange(cols_local, dtype=jnp.int32) // PANEL * col_groups + col
-
-    summed, rowp, colp, inverse, lower, solved = lead(layers, row_groups, col_groups)
-    rows = [rowp[p] for p in range(PANELS)]
-    cols = [colp[p] for p in range(PANELS)]
-    factors, left, right = [], [], []
-    for p in range(PANELS):
-        c_rows = jnp.where(own_block >= p, dot(rows[p], inverse[p], 1, 1), 0.0)
-        if p == 0:
-            c_rows = jnp.where(own_block == 0, lower, c_rows)
-        below = jnp.where(own_block > p, c_rows, 0.0)
-        c_cols = dot(inverse[p], cols[p], 1, 0)
-        c_cols = jnp.where((col_block > p)[None, :], c_cols, 0.0)
-        factors.append(c_rows)
-        left.append(below)
-        right.append(c_cols)
-        for q in range(p + 1, PANELS):
-            rows[q] = rows[q] - dot(below, solved, 1, 0)
-            cols[q] = cols[q] - dot(solved, c_cols, 0, 0)
-    update = dot(jnp.concatenate(left, 1), jnp.concatenate(right, 0), 1, 0)
-    schur = summed - update
-    factor = jnp.stack(factors)
-    width = PANEL // depth_groups
-    kept = lax.dynamic_slice_in_dim(factor, depth * width, width, 2)
-    sent = lax.dynamic_slice_in_dim(factor, (1 - depth) * width, width, 2)
-    got = lax.ppermute(sent, "depth", swap)
-    first = jnp.where(depth == 0, kept, got)
-    second = jnp.where(depth == 0, got, kept)
-    return jnp.concatenate([first, second], axis=1), schur
+    schur, factor = lead(layers, row_groups, col_groups)
+    return factor, schur
 
 
 def solution(mesh):

time: 130 us -> 114 us (0.88)
  the two profiles are of different devices: /device:TPU:25 before, /device:TPU:28 now
where the time goes in v3:
time: 114 us
  Pallas kernels  108 us (95%)
  local copies, waits for them, and re-layouts  4.52 us (4%)
    pallas_call x1, Pallas kernels, lead(): pl.pallas_call(functools.partial(lead_kernel, (row_groups, col_groups)),...  108 us
    unnamed x4, local copies, waits for them, and re-layouts  4.52 us

profile of v3, /device:TPU:28, one launch (start us, length us, event | category | flops | bytes accessed | tf_op | source)
XLA Modules:
  0.0 113.6 jit_solution(14942230414967973562)
XLA Ops:
  0.6 108.4 %lead.1 = (f32[512,1024]{1,0:T(8,128)}, f32[2,1024,256]{2,1,0:T(8,128)}) custom-call(f32[1,1024,1024]{2,1,0:T(8,128)} %layer.1), custom_call_target="tpu_custom_call" | custom-call | tf_op jit(solution)/shard_map/lead/pallas_call | solution.py:554
  109.1 0.0 copy-start
  109.1 3.2 %copy.5 = f32[2,1024,256]{2,1,0:T(8,128)} copy(f32[2,1024,256]{2,1,0:T(8,128)} %get-tuple-element.8) | data formatting | bytes 4194304
  112.3 0.0 copy-done
  112.3 1.3 %copy.6 = f32[512,1024]{1,0:T(8,128)} copy(f32[512,1024]{1,0:T(8,128)S(1)} %copy-done) | data formatting | bytes 4194304
Async XLA Ops:
  109.1 3.2 %copy-start = (f32[512,1024]{1,0:T(8,128)S(1)}, f32[512,1024]{1,0:T(8,128)}, u32[]{:S(2)}) copy-start(f32[512,1024]{1,0:T(8,128)} %get-tuple-element.9) | copy-start | bytes 6291460

commit v4 on v3

--- a/solution.py
+++ b/solution.py
@@ -436,18 +436,16 @@
     resume = max(base, reach)
     ticks(base, resume)
 
-    def landed(k, carry):
-        for item in range(PANELS):
+    def landed(item):
+        def step(k, carry):
             finish(*blocks_args(item, k), True)
-        return carry
-
-    lax.fori_loop(0, CHUNKS, landed, 0)
+            return carry
+
+        lax.fori_loop(0, CHUNKS, step, 0)
+
+    landed(0)
     solved[...] = dot(inverse[0], rest[0], 1, 0)
-
-    @pl.when((r == 1) & (d == 0))
-    def _():
-        lower[...] = solved[...].T
-
+    landed(1)
     whole = theirs.at[:, pl.ds(0, PANEL)]
     whole[...] = rest[1] - dot(solved[...], solved[...], 0, 0)
     for k in range(STEPS):
@@ -507,6 +505,10 @@
         factor[p, pl.ds(pl.multiple_of(d * PANEL, PANEL), PANEL), :] = kept
 
     def first_panel():
+        @pl.when((r == 1) & (d == 0))
+        def _():
+            lower[...] = solved[...].T
+
         tiles(PANEL, half, first_rows)
         arrived_cols(0)
         tiles(s_ref.shape[1], PANEL, first_cols)

time: 114 us -> 114 us (level)
  no operation moved by 1% of the time
where the time goes in v4:
time: 114 us
  Pallas kernels  109 us (96%)
  local copies, waits for them, and re-layouts  4.52 us (4%)
    pallas_call x1, Pallas kernels, lead(): pl.pallas_call(functools.partial(lead_kernel, (row_groups, col_groups)),...  109 us
    unnamed x4, local copies, waits for them, and re-layouts  4.52 us

profile of v4, /device:TPU:28, one launch (start us, length us, event | category | flops | bytes accessed | tf_op | source)
XLA Modules:
  0.0 113.8 jit_solution(16982898442810820812)
XLA Ops:
  0.6 108.6 %lead.1 = (f32[512,1024]{1,0:T(8,128)}, f32[2,1024,256]{2,1,0:T(8,128)}) custom-call(f32[1,1024,1024]{2,1,0:T(8,128)} %layer.1), custom_call_target="tpu_custom_call" | custom-call | tf_op jit(solution)/shard_map/lead/pallas_call | solution.py:556
  109.3 0.0 copy-start
  109.3 3.2 %copy.5 = f32[2,1024,256]{2,1,0:T(8,128)} copy(f32[2,1024,256]{2,1,0:T(8,128)} %get-tuple-element.8) | data formatting | bytes 4194304
  112.5 0.0 copy-done
  112.5 1.3 %copy.6 = f32[512,1024]{1,0:T(8,128)} copy(f32[512,1024]{1,0:T(8,128)S(1)} %copy-done) | data formatting | bytes 4194304
Async XLA Ops:
  109.3 3.2 %copy-start = (f32[512,1024]{1,0:T(8,128)S(1)}, f32[512,1024]{1,0:T(8,128)}, u32[]{:S(2)}) copy-start(f32[512,1024]{1,0:T(8,128)} %get-tuple-element.9) | copy-start | bytes 6291460
